TPU v7x, 32 devices: a whole 2x2x4 slice. The times are simulated.
32 devices in a mesh: groups: 2 (over x), gx: 16 (over z, y, core).
Axes of the slice: x: 2, y: 2, z: 4, core: 2. Of those that a mesh axis runs over, the one named last changes fastest.
Arguments:
- points: bfloat16 [32, 6, 1, 128, 512], P(('groups', 'gx')), parts along dimension 0, may hold values from -6 to 6
- order: int32 [32, 6, 1, 128], P(('groups', 'gx')), parts along dimension 0, may hold values from 0 to 127, each once within a row
- masks: int32 [32, 6, 1, 26], P(('groups', 'gx')), parts along dimension 0, may hold values 0 or 1
- counts: int32 [32, 6, 1], P('groups'), parts along dimension 0, may hold values from 1 to 128
- gain: float32 [512], replicated, may hold values from 0.5 to 1.5
- shift_bias: float32 [512], replicated, may hold values from -3 to 3
- w_qkv: bfloat16 [512, 1536], replicated, may hold values from -1.5 to 1.5
- w_out: bfloat16 [512, 512], replicated, may hold values from -0.25 to 0.25
Outputs:
- result: bfloat16 [32, 6, 1, 128, 512], P(('groups', 'gx')), parts along dimension 0
There are 2 independent parts, one for each index of `groups`. A program takes and returns all parts, laid end to end along the dimension named above; an argument that names none is the same for every part. Nothing has to cross between parts.
All inputs are finite; a program needn't handle non-finite values. No bound on the sum of `masks` on one device may be relied on, other than what follows from the above.
Results may differ from a plain program's by a relative error of at most 0.012.
Values may be sent and summed in bfloat16 or wider, within the bound.
A program may use at most 128 MiB of HBM per device.

v0:
```python
import functools

import jax
import jax.numpy as jnp
from jax import lax
from jax.experimental import pallas as pl
from jax.experimental.pallas import tpu as pltpu
from jax.sharding import PartitionSpec as P

HEADS = 8
TILE = 256
PIECE = 32
SPAN = 4
NEG = -1e30


def column_of(a, b, c):
    index = 9 * (a + 1) + 3 * (b + 1) + (c + 1)
    return index if index < 13 else index - 1


def reach(by, bz):
    spans = [(b, c) for b in (0, -1, 1) for c in (0, -1, 1)]
    return [o for o in spans if (by > 1 or o[0] == 0) and (bz > 1 or o[1] == 0)]


def norm_kernel(dims, pts_hbm, order_hbm, gain_hbm, shift_hbm, w_hbm, w_out_hbm, tiled_ref,
                normed_ref, w_ref, w_out_ref, pts_ref, order_ref, gain_ref, shift_ref, pts_sem,
                sems):
    by, bz, p, width, n = dims
    nb = by * bz
    copies = [
        pltpu.make_async_copy(order_hbm, order_ref, sems.at[0]),
        pltpu.make_async_copy(gain_hbm, gain_ref, sems.at[1]),
        pltpu.make_async_copy(shift_hbm, shift_ref, sems.at[2]),
    ]
    copies += [
        pltpu.make_async_copy(pts_hbm.at[g], pts_ref.at[g], pts_sem.at[g]) for g in range(nb)
    ]
    later = [
        pltpu.make_async_copy(w_hbm, w_ref, sems.at[3]),
        pltpu.make_async_copy(w_out_hbm, w_out_ref, sems.at[4]),
    ]
    for copy in copies + later:
        copy.start()
    for copy in copies:
        copy.wait()
    for g in range(nb):
        row = order_ref[0, g // bz, g % bz : g % bz + 1, :]
        pick = lax.broadcasted_iota(jnp.int32, (p, p), 0) == row
        pick = jnp.where(pick, 1.0, 0.0).astype(jnp.bfloat16)
        tiled = lax.dot_general(
            pick, pts_ref[g], (((0,), (0,)), ((), ())), preferred_element_type=jnp.float32
        )
        tiled_ref[g] = tiled.astype(jnp.bfloat16)
        mean = jnp.mean(tiled, axis=-1, keepdims=True)
        away = tiled - mean
        var = jnp.mean(away * away, axis=-1, keepdims=True)
        normed = away * lax.rsqrt(var + 1e-05) * gain_ref[...] + shift_ref[...]
        normed_ref[g * p : (g + 1) * p, :] = normed.astype(jnp.bfloat16)
    for copy in later:
        copy.wait()


def project(normed_ref, w_ref, lo, hi, put):
    for col in range(lo, hi, TILE):
        part = jnp.dot(
            normed_ref[...], w_ref[:, col : col + TILE], preferred_element_type=jnp.float32
        )
        put(col, part)


def put_keys(kv_ref, base, width):
    def put(col, part):
        rows = part.shape[0]
        kv_ref[base : base + rows, col - width : col - width + TILE] = part.astype(jnp.bfloat16)

    return put


def plan(slabs, masks_ref, counts_ref, table_ref, owner_ref, by, bz, p):
    nb = by * bz
    counts = [
        [jnp.where(present, counts_ref[k // bz, k % bz, at], 0) for k in range(nb)]
        for _, at, present in slabs
    ]
    item = jnp.int32(0)
    for g in range(nb):
        j, l = g // bz, g % bz
        base = item * SPAN
        used = base
        near = [(b, c) for b, c in reach(by, bz) if 0 <= j + b < by and 0 <= l + c < bz]
        for s, (kind, _, _) in enumerate(slabs):
            for b, c in near:
                k = (j + b) * bz + l + c
                count = counts[s][k]
                if kind is not None:
                    col = jnp.where(kind, column_of(1, b, c), column_of(-1, b, c))
                    count = count * masks_ref[0, j, l, col]
                elif (b, c) != (0, 0):
                    count = count * masks_ref[0, j, l, column_of(0, b, c)]
                for t in range(p // PIECE):
                    table_ref[0, used + t] = (s * nb + k) * p + t * PIECE
                    table_ref[1, used + t] = count - t * PIECE
                used = used + lax.shift_right_logical(count + (PIECE - 1), PIECE.bit_length() - 1)
        for t in range(SPAN):
            table_ref[0, used + t] = 0
            table_ref[1, used + t] = 0
        most = len(slabs) * len(near) * (p // PIECE) // SPAN
        for t in range(most):
            owner_ref[item + t] = g
        item = item + lax.shift_right_logical(used - base + (SPAN - 1), SPAN.bit_length() - 1)
    for t in range(2):
        owner_ref[item + t] = nb - 1
        for k in range(SPAN):
            table_ref[0, (item + t) * SPAN + k] = 0
            table_ref[1, (item + t) * SPAN + k] = 0
    return item


def work(items, table_ref, owner_ref, kv_ref, qd_ref, s_ref, m_ref, l_ref, acc_ref, width, p):
    hd = width // HEADS
    pairs = HEADS // 2

    def look(t):
        starts = [pl.multiple_of(table_ref[0, t * SPAN + k], PIECE) for k in range(SPAN)]
        return starts, [table_ref[1, t * SPAN + k] for k in range(SPAN)], owner_ref[t]

    def lanes_of(both, i):
        return jnp.concatenate([both[2 * i : 2 * i + 1], both[2 * i + 1 : 2 * i + 2]], axis=1)

    def scores(item, i):
        starts, limits, g = item
        place = lax.broadcasted_iota(jnp.int32, (PIECE, 2 * p), 0)
        bias = jnp.concatenate([jnp.where(place < c, 0.0, NEG) for c in limits], axis=0)
        cols = slice(2 * i * hd, 2 * (i + 1) * hd)
        keys = jnp.concatenate([kv_ref[pl.ds(a, PIECE), cols] for a in starts], axis=0)
        return jnp.dot(keys, qd_ref[g, i], preferred_element_type=jnp.float32) + bias

    def soften(state, i, s):
        tops, sums = state
        old = lanes_of(tops, i)
        top = jnp.maximum(old, jnp.max(s, axis=0, keepdims=True))
        keep = jnp.exp(old - top)
        e = jnp.exp(s - top)
        mass = lanes_of(sums, i) * keep + jnp.sum(e, axis=0, keepdims=True)
        return top, mass, keep, e.astype(jnp.bfloat16)

    def mix(item, i, e):
        vcols = slice(width + 2 * i * hd, width + 2 * (i + 1) * hd)
        values = jnp.concatenate([kv_ref[pl.ds(a, PIECE), vcols] for a in item[0]], axis=0)
        return lax.dot_general(
            values, e, (((0,), (0,)), ((), ())), preferred_element_type=jnp.float32
        )

    def put(item, i, soft, out):
        g = item[2]
        top, mass, keep, _ = soft
        for k in range(2):
            h = 2 * i + k
            lanes = slice(k * p, (k + 1) * p)
            down = slice(h * hd, (h + 1) * hd)
            acc_ref[g, down, :] = acc_ref[g, down, :] * keep[:, lanes] + out[k * hd : (k + 1) * hd, lanes]
            l_ref[g, h : h + 1, :] = mass[:, lanes]
            m_ref[g, h : h + 1, :] = top[:, lanes]

    def finish(item, state, read, ahead):
        last = None
        for i in range(pairs):
            ahead(i)
            soft = soften(state, i, read(i))
            out = mix(item, i, soft[3])
            if last is not None:
                put(item, *last)
            last = (i, soft, out)
        put(item, *last)

    def store(item):
        def ahead(i):
            s_ref[i] = scores(item, i)

        return ahead

    def two(u, carry):
        one, other, after = look(2 * u), look(2 * u + 1), look(2 * u + 2)
        held = {}

        def hold(i):
            held[i] = scores(other, i)

        finish(one, (m_ref[one[2]], l_ref[one[2]]), lambda i: s_ref[i], hold)
        finish(other, (m_ref[other[2]], l_ref[other[2]]), lambda i: held[i], store(after))
        return carry

    first = store(look(0))
    for i in range(pairs):
        first(i)
    lax.fori_loop(0, lax.shift_right_logical(items + 1, 1), two, 0)


def near_kernel(dims, masks_hbm, counts_hbm, normed_ref, pair_ref, w_ref, qd_ref, acc_ref, m_ref,
                l_ref, kv_ref, s_ref, table_ref, owner_ref, masks_ref, counts_ref, sems):
    by, bz, p, width, n = dims
    nb = by * bz
    hd = width // HEADS
    copies = [
        pltpu.make_async_copy(masks_hbm, masks_ref, sems.at[0]),
        pltpu.make_async_copy(counts_hbm, counts_ref, sems.at[1]),
    ]
    for copy in copies:
        copy.start()
    me = lax.axis_index("gx")
    even = me % 2 == 0
    blank = jnp.zeros((hd, p), jnp.bfloat16)
    acc_ref[...] = jnp.zeros_like(acc_ref)
    l_ref[...] = jnp.zeros_like(l_ref)
    m_ref[...] = jnp.full_like(m_ref, NEG)

    def put_q(col, part):
        part = part.astype(jnp.bfloat16) * jnp.bfloat16(1.0 / hd**0.5)
        for g in range(nb):
            turned = part[g * p : (g + 1) * p, :].T
            for h in range(TILE // hd):
                i, k = (col // hd + h) // 2, h % 2
                down = slice(k * hd, (k + 1) * hd)
                qd_ref[g, i, down, k * p : (k + 1) * p] = turned[h * hd : (h + 1) * hd, :]
                qd_ref[g, i, down, (1 - k) * p : (2 - k) * p] = blank

    project(normed_ref, w_ref, 0, width, put_q)
    for copy in copies:
        copy.wait()
    other = jnp.where(even, me + 1, me - 1)
    present = (other >= 0) & (other < n)
    slabs = [(None, me, True), (even, jnp.clip(other, 0, n - 1), present)]
    items = plan(slabs, masks_ref, counts_ref, table_ref, owner_ref, by, bz, p)
    project(normed_ref, w_ref, width, 3 * width, put_keys(kv_ref, 0, width))
    project(pair_ref, w_ref, width, 3 * width, put_keys(kv_ref, nb * p, width))
    work(items, table_ref, owner_ref, kv_ref, qd_ref, s_ref, m_ref, l_ref, acc_ref, width, p)


def far_kernel(dims, masks_hbm, counts_hbm, far_ref, w_ref, w_out_ref, tiled_ref, qd_ref,
               acc_in, m_in, l_in, out_hbm, acc_ref, m_ref, l_ref, attn_ref, out_ref, kv_ref, s_ref,
               table_ref, owner_ref, masks_ref, counts_ref, sems):
    by, bz, p, width, n = dims
    nb = by * bz
    hd = width // HEADS
    copies = [
        pltpu.make_async_copy(masks_hbm, masks_ref, sems.at[0]),
        pltpu.make_async_copy(counts_hbm, counts_ref, sems.at[1]),
    ]
    for copy in copies:
        copy.start()
    me = lax.axis_index("gx")
    even = me % 2 == 0
    project(far_ref, w_ref, width, 2 * width, put_keys(kv_ref, 0, width))
    for copy in copies:
        copy.wait()
    other = jnp.where(even, me - 1, me + 1)
    present = (other >= 0) & (other < n)
    slabs = [(jnp.logical_not(even), jnp.clip(other, 0, n - 1), present)]
    items = plan(slabs, masks_ref, counts_ref, table_ref, owner_ref, by, bz, p)
    project(far_ref, w_ref, 2 * width, 3 * width, put_keys(kv_ref, 0, width))
    work(items, table_ref, owner_ref, kv_ref, qd_ref, s_ref, m_ref, l_ref, acc_ref, width, p)
    row = lax.broadcasted_iota(jnp.int32, (p, width), 0)
    ends = []
    for lo in range(0, nb, 3):
        some = range(lo, min(lo + 3, nb))
        for g in some:
            inverse = 1.0 / l_ref[g]
            parts = [
                (acc_ref[g, h * hd : (h + 1) * hd, :] * inverse[h : h + 1, :]).astype(jnp.bfloat16)
                for h in range(HEADS)
            ]
            attn_ref[g * p : (g + 1) * p, :] = jnp.concatenate(parts, axis=0).T
        mixed = jnp.dot(
            attn_ref[lo * p : (lo + len(some)) * p, :], w_out_ref[...],
            preferred_element_type=jnp.float32,
        )
        for k, g in enumerate(some):
            part = mixed[k * p : (k + 1) * p] + tiled_ref[g].astype(jnp.float32)
            part = jnp.where(row < counts_ref[g // bz, g % bz, me], part, 0.0)
            out_ref[g] = part.astype(jnp.bfloat16)
        held = pl.ds(lo, len(some))
        end = pltpu.make_async_copy(out_ref.at[held], out_hbm.at[held], sems.at[2 + lo // 3])
        end.start()
        ends.append(end)
    for end in ends:
        end.wait()


def shards(points, order, masks, counts, gain, shift_bias, w_qkv, w_out):
    _, by, bz, p, width = points.shape
    n = lax.axis_size("gx")
    nb = by * bz
    dims = (by, bz, p, width, n)
    pairs = [e for i in range(0, n - 1, 2) for e in ((i, i + 1), (i + 1, i))]
    across = [e for i in range(1, n - 1, 2) for e in ((i, i + 1), (i + 1, i))]
    counts = counts.transpose(1, 2, 0)
    pin = lambda value: pltpu.with_memory_space_constraint(value, pltpu.HBM)
    masks, counts = pin(masks), pin(counts)
    shape = jax.ShapeDtypeStruct
    dma = pltpu.SemaphoreType.DMA
    vmem = pl.BlockSpec(memory_space=pltpu.VMEM)
    hbm = pl.BlockSpec(memory_space=pltpu.HBM)
    tiled, normed, w_here, w_out_here = pl.pallas_call(
        functools.partial(norm_kernel, dims),
        name="norm",
        out_shape=[
            shape((nb, p, width), jnp.bfloat16),
            shape((nb * p, width), jnp.bfloat16),
            shape(w_qkv.shape, jnp.bfloat16),
            shape(w_out.shape, jnp.bfloat16),
        ],
        in_specs=[hbm] * 6,
        out_specs=[vmem] * 4,
        scratch_shapes=[
            pltpu.VMEM((nb, p, width), jnp.bfloat16),
            pltpu.VMEM(order.shape, jnp.int32),
            pltpu.VMEM((1, width), jnp.float32),
            pltpu.VMEM((1, width), jnp.float32),
            dma((nb,)),
            dma((5,)),
        ],
        cost_estimate=pl.CostEstimate(
            flops=2 * nb * p * p * width, transcendentals=0, bytes_accessed=2 << 20
        ),
        compiler_params=pltpu.CompilerParams(vmem_limit_bytes=24 << 20),
    )(
        pin(points.reshape(nb, p, width)),
        pin(order),
        pin(gain.reshape(1, width)),
        pin(shift_bias.reshape(1, width)),
        pin(w_qkv),
        pin(w_out),
    )
    far = lax.ppermute(normed, "gx", across)
    pair = lax.ppermute(normed, "gx", pairs)
    slots = len(reach(by, bz))

    def scratch(slabs):
        most = nb * slabs * slots * (p // PIECE) + 4 * SPAN
        return [
            pltpu.VMEM((slabs * nb * p, 2 * width), jnp.bfloat16),
            pltpu.VMEM((HEADS // 2, PIECE * SPAN, 2 * p), jnp.float32),
            pltpu.SMEM((2, most), jnp.int32),
            pltpu.SMEM((most // SPAN,), jnp.int32),
            pltpu.SMEM(masks.shape, jnp.int32),
            pltpu.SMEM(counts.shape, jnp.int32),
        ]

    state = [
        shape((nb, width, p), jnp.float32),
        shape((nb, HEADS, p), jnp.float32),
        shape((nb, HEADS, p), jnp.float32),
    ]
    qd, acc, tops, sums = pl.pallas_call(
        functools.partial(near_kernel, dims),
        name="near",
        out_shape=[shape((nb, HEADS // 2, width // HEADS * 2, 2 * p), jnp.bfloat16)] + state,
        in_specs=[hbm, hbm, vmem, vmem, vmem],
        out_specs=[vmem] * 4,
        scratch_shapes=scratch(2) + [dma((2,))],
        cost_estimate=pl.CostEstimate(
            flops=8 * nb * p * width * 5 * width, transcendentals=0, bytes_accessed=8 << 20
        ),
        compiler_params=pltpu.CompilerParams(vmem_limit_bytes=40 << 20),
    )(masks, counts, normed, pair, w_here)
    out = pl.pallas_call(
        functools.partial(far_kernel, dims),
        name="far",
        out_shape=[shape((nb, p, width), jnp.bfloat16)] + state,
        in_specs=[hbm, hbm] + [vmem] * 8,
        out_specs=[hbm] + [vmem] * 3,
        scratch_shapes=[
            pltpu.VMEM((nb * p, width), jnp.bfloat16),
            pltpu.VMEM((nb, p, width), jnp.bfloat16),
        ]
        + scratch(1)
        + [dma((2 + -(-nb // 3),))],
        input_output_aliases={7: 1, 8: 2, 9: 3},
        cost_estimate=pl.CostEstimate(
            flops=4 * nb * p * width * 3 * width, transcendentals=0, bytes_accessed=8 << 20
        ),
        compiler_params=pltpu.CompilerParams(vmem_limit_bytes=40 << 20),
    )(masks, counts, far, w_here, w_out_here, tiled, qd, acc, tops, sums)[0]
    return out.reshape(points.shape)


def solution(mesh):
    placed = (
        P(("groups", "gx"), None, None, None, None),
        P(("groups", "gx"), None, None, None),
        P(("groups", "gx"), None, None, None),
        P("groups", None, None),
        P(),
        P(),
        P(),
        P(),
    )
    return jax.shard_map(
        shards,
        mesh=mesh,
        in_specs=placed,
        out_specs=P(("groups", "gx"), None, None, None, None),
        check_vma=False,
    )
```

profile of v0, /device:TPU:25, one launch (start us, length us, event | category | flops | bytes accessed | tf_op | source)
XLA Modules:
  0.0 30.1 jit_solution(16198135131415781218)
XLA Ops:
  0.0 2.6 %norm.1 = (bf16[6,128,512]{2,1,0:T(8,128)(2,1)S(1)}, bf16[768,512]{1,0:T(8,128)(2,1)S(1)}, bf16[512,1536]{1,0:T(8,128)(2,1)S(1)}, bf16[512,512]{1,0:T(8,128)(2,1)S(1)}) custom-call(bf16[6,128,512]{2,1,0:T(8,128)(2,1)} %bitcast.7, s32[1,6,1,128]{3,2,1,0:T(1,128)} %order_hbm.1, f32[1,512]{1,0:T(1,128)} %bitcast.8, f32[1,512]{1,0:T(1,128)} %bitcast.9, ...), custom_call_target="tpu_custom_call" | custom-call | flops 100663296 | bytes 2097152 | tf_op jit(solution)/shard_map/norm/pallas_call | solution.py:305
  2.6 0.7 %collective-permute-start.1 = (bf16[768,512]{1,0:T(8,128)(2,1)S(1)}, bf16[768,512]{1,0:T(8,128)(2,1)S(1)}, u32[]{:S(2)}, u32[]{:S(2)}) collective-permute-start(bf16[768,512]{1,0:T(8,128)(2,1)S(1)} %get-tuple-element.14.normed_ref), channel_id=1, source_target_pairs={{0,1},{1,0},{2,3},{3,2},{4,5},{5,4},{6,7},{7,6},{8,9},{9,8},{10,11... | collective-permute-start | bytes 2359304 | tf_op jit(solution)/shard_map/ppermute | solution.py:337
  3.3 3.0 %collective-permute-start = (bf16[768,512]{1,0:T(8,128)(2,1)S(1)}, bf16[768,512]{1,0:T(8,128)(2,1)S(1)}, u32[]{:S(2)}, u32[]{:S(2)}) collective-permute-start(bf16[768,512]{1,0:T(8,128)(2,1)S(1)} %get-tuple-element.14.normed_ref), channel_id=1, source_target_pairs={{1,2},{2,1},{3,4},{4,3},{5,6},{6,5},{7,8},{8,7},{9,10},{10,9},{11,... | collective-permute-start | bytes 2359304 | tf_op jit(solution)/shard_map/ppermute | solution.py:336
  6.4 0.0 collective-permute-done.1.pair_ref
  6.4 6.4 %near.1 = (bf16[6,4,128,256]{3,2,1,0:T(8,128)(2,1)S(1)}, f32[6,512,128]{2,1,0:T(8,128)S(1)}, f32[6,8,128]{2,1,0:T(8,128)S(1)}, f32[6,8,128]{2,1,0:T(8,128)S(1)}) custom-call(s32[1,6,1,26]{3,2,1,0:T(1,128)} %masks_hbm.3, s32[6,1,16]{2,1,0:T(1,128)} %bitcast.10, bf16[768,512]{1,0:T(8,128)(2,1)S(1)} %get-tuple-element.14.normed_ref, ...), custom_call_target="tpu_custom_call" | custom-call | flops 8053063680 | bytes 8388608 | tf_op jit(solution)/shard_map/near/pallas_call | solution.py:356
  12.8 12.2 %collective-permute-done.far_ref = bf16[768,512]{1,0:T(8,128)(2,1)S(1)} collective-permute-done((bf16[768,512]{1,0:T(8,128)(2,1)S(1)}, bf16[768,512]{1,0:T(8,128)(2,1)S(1)}, u32[]{:S(2)}, u32[]{:S(2)}) %collective-permute-start) | collective-permute-done | bytes 786464 | tf_op jit(solution)/shard_map/ppermute | solution.py:336
  25.0 5.1 %far.1 = (bf16[6,128,512]{2,1,0:T(8,128)(2,1)}, f32[6,512,128]{2,1,0:T(8,128)S(1)}, f32[6,8,128]{2,1,0:T(8,128)S(1)}, f32[6,8,128]{2,1,0:T(8,128)S(1)}) custom-call(s32[1,6,1,26]{3,2,1,0:T(1,128)} %masks_hbm.3, s32[6,1,16]{2,1,0:T(1,128)} %bitcast.11, ...), custom_call_target="tpu_custom_call", output_to_operand_aliasing={{1}: (7, {}), {2}: (8, {}), {3}: (9, {})} | custom-call | flops 2415919104 | bytes 8388608 | tf_op jit(solution)/shard_map/far/pallas_call | solution.py:368
Async XLA Ops:
  2.6 3.8 %collective-permute-start.1 = (bf16[768,512]{1,0:T(8,128)(2,1)S(1)}, bf16[768,512]{1,0:T(8,128)(2,1)S(1)}, u32[]{:S(2)}, u32[]{:S(2)}) collective-permute-start(bf16[768,512]{1,0:T(8,128)(2,1)S(1)} %get-tuple-element.14.normed_ref), channel_id=1, source_target_pairs={{0,1},{1,0},{2,3},{3,2},{4,5},{5,4},{6,7},{7,6},{8,9},{9,8},{10,11... | collective-permute-start | bytes 2359304 | tf_op jit(solution)/shard_map/ppermute | solution.py:337
  3.3 21.7 %collective-permute-start = (bf16[768,512]{1,0:T(8,128)(2,1)S(1)}, bf16[768,512]{1,0:T(8,128)(2,1)S(1)}, u32[]{:S(2)}, u32[]{:S(2)}) collective-permute-start(bf16[768,512]{1,0:T(8,128)(2,1)S(1)} %get-tuple-element.14.normed_ref), channel_id=1, source_target_pairs={{1,2},{2,1},{3,4},{4,3},{5,6},{6,5},{7,8},{8,7},{9,10},{10,9},{11,... | collective-permute-start | bytes 2359304 | tf_op jit(solution)/shard_map/ppermute | solution.py:336
where the time goes:
time: 30.6 us; the launch traced here: 30.1 us
  Pallas kernels  14.1 us (46%)
  waiting for transfers between devices  12.2 us (40%)
  starting transfers between devices  3.79 us (12%)
    ppermute x1, waiting for transfers between devices, shards(): far = lax.ppermute(normed, 'gx', across)  12.2 us
    pallas_call x1, Pallas kernels, shards(): pl.pallas_call(functools.partial(near_kernel, dims), name='near', out_sha...  6.43 us
    pallas_call x1, Pallas kernels, shards(): pl.pallas_call(functools.partial(far_kernel, dims), name='far', out_shape...  5.11 us
    ppermute x1, starting transfers between devices, shards(): far = lax.ppermute(normed, 'gx', across)  3.05 us
    pallas_call x1, Pallas kernels, shards(): pl.pallas_call(functools.partial(norm_kernel, dims), name='norm', out_sha...  2.55 us
    ppermute x1, starting transfers between devices, shards(): pair = lax.ppermute(normed, 'gx', pairs)  0.74 us
  transfers between devices with their start and end apart: 2, of which 1 were waited for; matrix products, arithmetic and copies ran while one was open for 0% of the time, Pallas kernels for 21%

commit v1 on v0

v1 whole, which is shorter than its diff:
```python
import functools

import jax
import jax.numpy as jnp
from jax import lax
from jax.experimental import pallas as pl
from jax.experimental.pallas import tpu as pltpu
from jax.sharding import PartitionSpec as P

HEADS = 8
TILE = 256
NEG = -1e30
MESH = pl.DeviceIdType.MESH


def column_of(a, b, c):
    index = 9 * (a + 1) + 3 * (b + 1) + (c + 1)
    return index if index < 13 else index - 1


def reach(by, bz):
    spans = [(b, c) for b in (0, -1, 1) for c in (0, -1, 1)]
    return [o for o in spans if (by > 1 or o[0] == 0) and (bz > 1 or o[1] == 0)]


def spot(k, bz):
    return (k, 0) if bz == 1 else (k // bz, k % bz)


def arrange(order_ref, pts_ref, k, bz, gain_ref, shift_ref):
    p = pts_ref.shape[1]
    j, l = spot(k, bz)
    row = order_ref[0, j, pl.ds(l, 1), :]
    pick = lax.broadcasted_iota(jnp.int32, (p, p), 0) == row
    pick = jnp.where(pick, 1.0, 0.0).astype(jnp.bfloat16)
    tiled = lax.dot_general(
        pick, pts_ref[k], (((0,), (0,)), ((), ())), preferred_element_type=jnp.float32
    )
    mean = jnp.mean(tiled, axis=-1, keepdims=True)
    away = tiled - mean
    var = jnp.mean(away * away, axis=-1, keepdims=True)
    normed = away * lax.rsqrt(var + 1e-05) * gain_ref[...] + shift_ref[...]
    return tiled.astype(jnp.bfloat16), normed.astype(jnp.bfloat16)


def project(normed_ref, w_ref, lo, hi, put):
    for col in range(lo, hi, TILE):
        part = jnp.dot(
            normed_ref[...], w_ref[:, col : col + TILE], preferred_element_type=jnp.float32
        )
        put(col, part)


def put_keys(kv_ref, s, width):
    def put(col, part):
        nb, p = kv_ref.shape[1:3]
        part = part.astype(jnp.bfloat16).reshape(nb, p, TILE)
        kv_ref[s, :, :, col - width : col - width + TILE] = part

    return put


def flow(rounds, items, kv_ref, qd_ref, s_ref, limit_ref, m_ref, l_ref, acc_ref, width, p):
    hd = width // HEADS
    pairs = HEADS // 2

    def lanes_of(both, i):
        return jnp.concatenate([both[2 * i : 2 * i + 1], both[2 * i + 1 : 2 * i + 2]], axis=1)

    def scores(item, i):
        s, k, g, at = item
        place = lax.broadcasted_iota(jnp.int32, (p, 2 * p), 0)
        bias = jnp.where(place < limit_ref[at], 0.0, NEG)
        keys = kv_ref[s, k, :, 2 * i * hd : 2 * (i + 1) * hd]
        return jnp.dot(keys, qd_ref[g, i], preferred_element_type=jnp.float32) + bias

    def soften(state, i, s):
        tops, sums = state
        old = lanes_of(tops, i)
        top = jnp.maximum(old, jnp.max(s, axis=0, keepdims=True))
        keep = jnp.exp(old - top)
        e = jnp.exp(s - top)
        mass = lanes_of(sums, i) * keep + jnp.sum(e, axis=0, keepdims=True)
        return top, mass, keep, e.astype(jnp.bfloat16)

    def mix(item, i, e):
        values = kv_ref[item[0], item[1], :, width + 2 * i * hd : width + 2 * (i + 1) * hd]
        return lax.dot_general(
            values, e, (((0,), (0,)), ((), ())), preferred_element_type=jnp.float32
        )

    def put(item, i, soft, out):
        g = item[2]
        top, mass, keep, _ = soft
        for k in range(2):
            h = 2 * i + k
            lanes = slice(k * p, (k + 1) * p)
            down = slice(h * hd, (h + 1) * hd)
            old = acc_ref[g, down, :] * keep[:, lanes]
            acc_ref[g, down, :] = old + out[k * hd : (k + 1) * hd, lanes]
            l_ref[g, h : h + 1, :] = mass[:, lanes]
            m_ref[g, h : h + 1, :] = top[:, lanes]

    def finish(item, read, ahead):
        state = m_ref[item[2]], l_ref[item[2]]
        last = None
        for i in range(pairs):
            ahead(i)
            soft = soften(state, i, read(i))
            out = mix(item, i, soft[3])
            if last is not None:
                put(item, *last)
            last = (i, soft, out)
        put(item, *last)

    def store(item):
        def ahead(i):
            s_ref[i] = scores(item, i)

        return ahead

    def one(u, carry):
        now = items(u)
        after = items((u + 1) % rounds)[0] if rounds > 1 else None
        held = [{} for _ in now]
        for t, item in enumerate(now):
            if t + 1 < len(now):
                ahead = lambda i, t=t: held[t + 1].update({i: scores(now[t + 1], i)})
            elif after is not None:
                ahead = store(after)
            else:
                ahead = lambda i: None
            read = (lambda i: s_ref[i]) if t == 0 else (lambda i, t=t: held[t][i])
            finish(item, read, ahead)
        return carry

    first = store(items(0)[0])
    for i in range(pairs):
        first(i)
    if rounds > 1:
        lax.fori_loop(0, rounds, one, 0)
    else:
        one(0, 0)


def main_kernel(dims, pts_hbm, order_hbm, masks_hbm, counts_hbm, gain_hbm, shift_hbm, w_hbm,
                w_out_hbm, tiled_ref, acc_ref, l_ref, live_ref, w_out_ref, pts_ref, order_ref,
                normed_ref, block_ref, kv_ref, qd_ref, s_ref, m_ref, gain_ref, shift_ref, w_ref, limit_ref,
                masks_ref, counts_ref, sems, own_sem, pair_send, pair_recv, far_send, far_recv):
    by, bz, p, width, n = dims
    nb = by * bz
    hd = width // HEADS
    me = lax.axis_index("gx")
    odd = me % 2
    pair = me + 1 - 2 * odd
    far = me - 1 + 2 * odd
    has = (far >= 0) & (far < n)
    barrier = pltpu.get_barrier_semaphore()
    pl.semaphore_signal(barrier, inc=1, device_id={"gx": pair}, device_id_type=MESH)

    @pl.when(has)
    def _():
        pl.semaphore_signal(barrier, inc=1, device_id={"gx": far}, device_id_type=MESH)

    small = [
        pltpu.make_async_copy(order_hbm, order_ref.at[0], sems.at[0]),
        pltpu.make_async_copy(gain_hbm, gain_ref, sems.at[1]),
        pltpu.make_async_copy(shift_hbm, shift_ref, sems.at[2]),
        pltpu.make_async_copy(masks_hbm, masks_ref, sems.at[3]),
        pltpu.make_async_copy(counts_hbm, counts_ref, sems.at[4]),
    ]
    own = pltpu.make_async_copy(pts_hbm, pts_ref.at[0], own_sem)
    weights = pltpu.make_async_copy(w_hbm, w_ref, sems.at[5])
    weights_out = pltpu.make_async_copy(w_out_hbm, w_out_ref, sems.at[6])
    for copy in small + [own, weights, weights_out]:
        copy.start()

    def send(source, target, out_sem, in_sem, device):
        return pltpu.make_async_remote_copy(
            src_ref=source, dst_ref=target, send_sem=out_sem, recv_sem=in_sem,
            device_id={"gx": device}, device_id_type=MESH,
        )

    def far_block(k):
        return send(pts_hbm.at[k], pts_ref.at[2, k], far_send.at[k], far_recv.at[k], far)

    far_order = send(order_hbm, order_ref.at[2], far_send.at[nb], far_recv.at[nb], far)
    pair_order = send(order_hbm, order_ref.at[1], pair_send.at[0], pair_recv.at[0], pair)
    pair_points = send(pts_hbm, pts_ref.at[1], pair_send.at[1], pair_recv.at[1], pair)

    @pl.when(has)
    def _():
        pl.semaphore_wait(barrier, 2)

    @pl.when(jnp.logical_not(has))
    def _():
        pl.semaphore_wait(barrier, 1)

    @pl.when(has)
    def _():
        far_order.start()
        for k in range(nb):
            far_block(k).start()

    pair_order.start()
    pair_points.start()

    for copy in small:
        copy.wait()
    near = reach(by, bz)
    reachable = len(near)
    here = has.astype(jnp.int32)
    slabs = [(me, 0, 1), (pair, 1 - 2 * odd, 1), ((far + n) % n, 2 * odd - 1, here)]
    for s, (at, _, there) in enumerate(slabs):
        for g in range(nb):
            j, l = spot(g, bz)
            for r, (b, c) in enumerate(near):
                inside = 0 <= j + b < by and 0 <= l + c < bz
                k = g + b * bz + c
                key = g if s < 2 else k % nb
                slot = (s * nb + key) * reachable + r
                if not inside:
                    limit_ref[slot] = 0
                    continue
                count = counts_ref[j + b, l + c, at] * there
                if s == 0 and (b, c) != (0, 0):
                    count = count * masks_ref[0, j, l, column_of(0, b, c)]
                if s > 0:
                    plus, minus = column_of(1, b, c), column_of(-1, b, c)
                    sign = 1 - odd if s == 1 else odd
                    count = count * masks_ref[0, j, l, minus + (plus - minus) * sign]
                limit_ref[slot] = count
    for g in range(nb):
        j, l = spot(g, bz)
        live_ref[g] = jnp.full(live_ref.shape[1:], counts_ref[j, l, me], jnp.int32)
    acc_ref[...] = jnp.zeros_like(acc_ref)
    l_ref[...] = jnp.zeros_like(l_ref)
    m_ref[...] = jnp.full_like(m_ref, NEG)

    own.wait()
    for g in range(nb):
        tiled, normed = arrange(order_ref.at[0], pts_ref.at[0], g, bz, gain_ref, shift_ref)
        tiled_ref[g] = tiled
        normed_ref[g * p : (g + 1) * p, :] = normed
    weights.wait()
    weights_out.wait()
    blank = jnp.zeros((hd, p), jnp.bfloat16)

    def put_q(col, part):
        part = part.astype(jnp.bfloat16) * jnp.bfloat16(1.0 / hd**0.5)
        for g in range(nb):
            turned = part[g * p : (g + 1) * p, :].T
            for h in range(TILE // hd):
                i, k = (col // hd + h) // 2, h % 2
                down = slice(k * hd, (k + 1) * hd)
                qd_ref[g, i, down, k * p : (k + 1) * p] = turned[h * hd : (h + 1) * hd, :]
                qd_ref[g, i, down, (1 - k) * p : (2 - k) * p] = blank

    project(normed_ref, w_ref, 0, width, put_q)
    project(normed_ref, w_ref, width, 3 * width, put_keys(kv_ref, 0, width))
    rest = (kv_ref, qd_ref, s_ref, limit_ref, m_ref, l_ref, acc_ref, width, p)

    def around(s):
        def items(g):
            return [
                (s, (g + b * bz + c + nb) % nb, g, (s * nb + g) * reachable + r)
                for r, (b, c) in enumerate(near)
            ]

        return items

    flow(nb, around(0), *rest)
    pair_order.wait_recv()
    pair_points.wait_recv()
    for g in range(nb):
        _, normed = arrange(order_ref.at[1], pts_ref.at[1], g, bz, gain_ref, shift_ref)
        normed_ref[g * p : (g + 1) * p, :] = normed
    project(normed_ref, w_ref, width, 3 * width, put_keys(kv_ref, 1, width))
    flow(nb, around(1), *rest)

    @pl.when(has)
    def _():
        far_order.wait_recv()

        def block(k, carry):
            far_block(k).wait_recv()
            _, normed = arrange(order_ref.at[2], pts_ref.at[2], k, bz, gain_ref, shift_ref)
            block_ref[...] = normed
            for col in range(width, 3 * width, TILE):
                part = jnp.dot(
                    block_ref[...], w_ref[:, col : col + TILE], preferred_element_type=jnp.float32
                )
                kv_ref[2, k, :, col - width : col - width + TILE] = part.astype(jnp.bfloat16)

            def items(u):
                return [
                    (2, k, (k - b * bz - c + nb) % nb, (2 * nb + k) * reachable + r)
                    for r, (b, c) in enumerate(near)
                ]

            flow(1, items, *rest)
            return carry

        lax.fori_loop(0, nb, block, 0)
        far_order.wait_send()
        for k in range(nb):
            far_block(k).wait_send()

    pair_order.wait_send()
    pair_points.wait_send()


def tail_kernel(dims, acc_ref, l_ref, tiled_ref, live_ref, w_out_ref, out_hbm, attn_ref, out_ref, sems):
    by, bz, p, width, n = dims
    nb = by * bz
    hd = width // HEADS
    row = lax.broadcasted_iota(jnp.int32, (p, width), 0)
    ends = []
    for lo in range(0, nb, 3):
        some = range(lo, min(lo + 3, nb))
        for g in some:
            inverse = 1.0 / l_ref[g]
            parts = [
                (acc_ref[g, h * hd : (h + 1) * hd, :] * inverse[h : h + 1, :]).astype(jnp.bfloat16)
                for h in range(HEADS)
            ]
            attn_ref[g * p : (g + 1) * p, :] = jnp.concatenate(parts, axis=0).T
        mixed = jnp.dot(
            attn_ref[lo * p : (lo + len(some)) * p, :], w_out_ref[...],
            preferred_element_type=jnp.float32,
        )
        for k, g in enumerate(some):
            part = mixed[k * p : (k + 1) * p] + tiled_ref[g].astype(jnp.float32)
            part = jnp.where(row < live_ref[g, :1, :], part, 0.0)
            out_ref[g] = part.astype(jnp.bfloat16)
        held = pl.ds(lo, len(some))
        end = pltpu.make_async_copy(out_ref.at[held], out_hbm.at[held], sems.at[lo // 3])
        end.start()
        ends.append(end)
    for end in ends:
        end.wait()


def shards(points, order, masks, counts, gain, shift_bias, w_qkv, w_out):
    _, by, bz, p, width = points.shape
    n = lax.axis_size("gx")
    nb = by * bz
    dims = (by, bz, p, width, n)
    counts = counts.transpose(1, 2, 0)
    pin = lambda value: pltpu.with_memory_space_constraint(value, pltpu.HBM)
    shape = jax.ShapeDtypeStruct
    dma = pltpu.SemaphoreType.DMA
    vmem = pl.BlockSpec(memory_space=pltpu.VMEM)
    hbm = pl.BlockSpec(memory_space=pltpu.HBM)
    half = jnp.bfloat16
    tiled, acc, sums, live, w_here = pl.pallas_call(
        functools.partial(main_kernel, dims),
        name="main",
        out_shape=[
            shape((nb, p, width), half),
            shape((nb, width, p), jnp.float32),
            shape((nb, HEADS, p), jnp.float32),
            shape((nb, 8, width), jnp.int32),
            shape(w_out.shape, half),
        ],
        in_specs=[hbm] * 8,
        out_specs=[vmem] * 5,
        scratch_shapes=[
            pltpu.VMEM((3, nb, p, width), half),
            pltpu.VMEM((3,) + order.shape, jnp.int32),
            pltpu.VMEM((nb * p, width), half),
            pltpu.VMEM((p, width), half),
            pltpu.VMEM((3, nb, p, 2 * width), half),
            pltpu.VMEM((nb, HEADS // 2, width // HEADS * 2, 2 * p), half),
            pltpu.VMEM((HEADS // 2, p, 2 * p), jnp.float32),
            pltpu.VMEM((nb, HEADS, p), jnp.float32),
            pltpu.VMEM((1, width), jnp.float32),
            pltpu.VMEM((1, width), jnp.float32),
            pltpu.VMEM(w_qkv.shape, half),
            pltpu.SMEM((3 * nb * len(reach(by, bz)),), jnp.int32),
            pltpu.SMEM(masks.shape, jnp.int32),
            pltpu.SMEM(counts.shape, jnp.int32),
            dma((7,)),
            dma,
            dma((2,)),
            dma((2,)),
            dma((nb + 1,)),
            dma((nb + 1,)),
        ],
        cost_estimate=pl.CostEstimate(
            flops=2 * nb * p * width * 24 * width, transcendentals=0, bytes_accessed=8 << 20
        ),
        compiler_params=pltpu.CompilerParams(
            vmem_limit_bytes=48 << 20, collective_id=0, has_side_effects=True
        ),
    )(
        pin(points.reshape(nb, p, width)),
        pin(order),
        pin(masks),
        pin(counts),
        pin(gain.reshape(1, width)),
        pin(shift_bias.reshape(1, width)),
        pin(w_qkv),
        pin(w_out),
    )
    out = pl.pallas_call(
        functools.partial(tail_kernel, dims),
        name="tail",
        out_shape=shape((nb, p, width), half),
        in_specs=[vmem] * 5,
        out_specs=hbm,
        scratch_shapes=[
            pltpu.VMEM((nb * p, width), half),
            pltpu.VMEM((nb, p, width), half),
            dma((-(-nb // 3),)),
        ],
        cost_estimate=pl.CostEstimate(
            flops=2 * nb * p * width * width, transcendentals=0, bytes_accessed=2 << 20
        ),
        compiler_params=pltpu.CompilerParams(vmem_limit_bytes=16 << 20),
    )(acc, sums, tiled, live, w_here)
    return out.reshape(points.shape)


def solution(mesh):
    placed = (
        P(("groups", "gx"), None, None, None, None),
        P(("groups", "gx"), None, None, None),
        P(("groups", "gx"), None, None, None),
        P("groups", None, None),
        P(),
        P(),
        P(),
        P(),
    )
    return jax.shard_map(
        shards,
        mesh=mesh,
        in_specs=placed,
        out_specs=P(("groups", "gx"), None, None, None, None),
        check_vma=False,
    )
```

time: 30.6 us -> 25.9 us (0.85)
  the two profiles are of different devices: /device:TPU:25 before, /device:TPU:1 now
where the time goes in v1:
time: 25.9 us; the launch traced here: 25.7 us
  Pallas kernels  25.7 us (99%)
    pallas_call x1, Pallas kernels, shards(): pl.pallas_call(functools.partial(main_kernel, dims), name='main', out_sha...  24.3 us
    pallas_call x1, Pallas kernels, shards(): pl.pallas_call(functools.partial(tail_kernel, dims), name='tail', out_sha...  1.46 us

profile of v1, /device:TPU:1, one launch (start us, length us, event | category | flops | bytes accessed | tf_op | source)
XLA Modules:
  0.0 25.7 jit_solution(13488058775071004596)
XLA Ops:
  0.0 24.3 %main.1 = (bf16[6,128,512]{2,1,0:T(8,128)(2,1)S(1)}, f32[6,512,128]{2,1,0:T(8,128)S(1)}, f32[6,8,128]{2,1,0:T(8,128)S(1)}, s32[6,8,512]{2,1,0:T(8,128)S(1)}, bf16[512,512]{1,0:T(8,128)(2,1)S(1)}) custom-call(bf16[6,128,512]{2,1,0:T(8,128)(2,1)} %bitcast.7, s32[1,6,1,128]{3,2,1,0:T(1,128)} %order_hbm.1, s32[1,6,1,26]{3,2,1,0:T(1,128)} %masks_hbm.1, ...), custom_call_target="tpu_custom_call" | custom-call | flops 9663676416 | bytes 8388608 | tf_op jit(solution)/shard_map/main/pallas_call | solution.py:356
  24.3 1.5 %tail.1 = bf16[6,128,512]{2,1,0:T(8,128)(2,1)} custom-call(f32[6,512,128]{2,1,0:T(8,128)S(1)} %get-tuple-element.10.acc_ref, f32[6,8,128]{2,1,0:T(8,128)S(1)} %get-tuple-element.11.l_ref, bf16[6,128,512]{2,1,0:T(8,128)(2,1)S(1)} %get-tuple-element.12.tiled_ref, s32[6,8,512]{2,1,0:T(8,128)S(1)} %get-tuple-element.13.live_ref, ...), custom_call_target="tpu_custom_call" | custom-call | flops 402653184 | bytes 2097152 | tf_op jit(solution)/shard_map/tail/pallas_call | solution.py:406

commit v2 on v1

--- a/solution.py
+++ b/solution.py
@@ -19,8 +19,21 @@
 
 
 def reach(by, bz):
-    spans = [(b, c) for b in (0, -1, 1) for c in (0, -1, 1)]
+    spans = [(b, c) for b in (-1, 0, 1) for c in (-1, 0, 1)]
     return [o for o in spans if (by > 1 or o[0] == 0) and (bz > 1 or o[1] == 0)]
+
+
+def links(by, bz, k, side):
+    nb = by * bz
+    found = []
+    for r, (b, c) in enumerate(reach(by, bz)):
+        if isinstance(k, int):
+            j, l = k // bz + side * b, k % bz + side * c
+            if not (0 <= j < by and 0 <= l < bz):
+                continue
+        other = (k + side * (b * bz + c) + nb) % nb
+        found.append((r, k, other))
+    return found
 
 
 def spot(k, bz):
@@ -262,46 +275,56 @@
 
     def around(s):
         def items(g):
-            return [
-                (s, (g + b * bz + c + nb) % nb, g, (s * nb + g) * reachable + r)
-                for r, (b, c) in enumerate(near)
-            ]
-
-        return items
-
-    flow(nb, around(0), *rest)
+            return [(s, k, g, (s * nb + g) * reachable + r) for r, g, k in links(by, bz, g, 1)]
+
+        def row(u):
+            places = [u * per + t + 1 for t in range(per)]
+            return [(s, v // 3 + v % 3 - 1, v // 3, s * nb * 3 + v) for v in places]
+
+        if bz > 1 or by == 1:
+            return nb, items
+        per = max(d for d in (1, 2, 4) if (3 * nb - 2) % d == 0)
+        return (3 * nb - 2) // per, row
+
+    flow(*around(0), *rest)
     pair_order.wait_recv()
     pair_points.wait_recv()
     for g in range(nb):
         _, normed = arrange(order_ref.at[1], pts_ref.at[1], g, bz, gain_ref, shift_ref)
         normed_ref[g * p : (g + 1) * p, :] = normed
     project(normed_ref, w_ref, width, 3 * width, put_keys(kv_ref, 1, width))
-    flow(nb, around(1), *rest)
+    flow(*around(1), *rest)
+
+    def fetch(k, between):
+        far_block(k).wait_recv()
+        _, normed = arrange(order_ref.at[2], pts_ref.at[2], k, bz, gain_ref, shift_ref)
+        block_ref[...] = normed
+        between()
+        for col in range(width, 3 * width, TILE):
+            part = jnp.dot(
+                block_ref[...], w_ref[:, col : col + TILE], preferred_element_type=jnp.float32
+            )
+            kv_ref[2, k, :, col - width : col - width + TILE] = part.astype(jnp.bfloat16)
+
+    def served(k):
+        def items(u):
+            return [(2, k, g, (2 * nb + k) * reachable + r) for r, k, g in links(by, bz, k, -1)]
+
+        flow(1, items, *rest)
 
     @pl.when(has)
     def _():
         far_order.wait_recv()
-
-        def block(k, carry):
-            far_block(k).wait_recv()
-            _, normed = arrange(order_ref.at[2], pts_ref.at[2], k, bz, gain_ref, shift_ref)
-            block_ref[...] = normed
-            for col in range(width, 3 * width, TILE):
-                part = jnp.dot(
-                    block_ref[...], w_ref[:, col : col + TILE], preferred_element_type=jnp.float32
-                )
-                kv_ref[2, k, :, col - width : col - width + TILE] = part.astype(jnp.bfloat16)
-
-            def items(u):
-                return [
-                    (2, k, (k - b * bz - c + nb) % nb, (2 * nb + k) * reachable + r)
-                    for r, (b, c) in enumerate(near)
-                ]
-
-            flow(1, items, *rest)
+        fetch(0, lambda: None)
+        if nb > 1:
+            fetch(1, lambda: served(0))
+
+        def step(k, carry):
+            fetch(k, lambda: served(k - 1))
             return carry
 
-        lax.fori_loop(0, nb, block, 0)
+        lax.fori_loop(2, nb, step, 0)
+        served(nb - 1)
         far_order.wait_send()
         for k in range(nb):
             far_block(k).wait_send()

time: 25.9 us -> 23.9 us (0.923)
  the two profiles are of different devices: /device:TPU:1 before, /device:TPU:25 now
where the time goes in v2:
time: 23.9 us; the launch traced here: 23.8 us
  Pallas kernels  23.8 us (100%)
    pallas_call x1, Pallas kernels, shards(): pl.pallas_call(functools.partial(main_kernel, dims), name='main', out_sha...  22.3 us
    pallas_call x1, Pallas kernels, shards(): pl.pallas_call(functools.partial(tail_kernel, dims), name='tail', out_sha...  1.46 us

profile of v2, /device:TPU:25, one launch (start us, length us, event | category | flops | bytes accessed | tf_op | source)
XLA Modules:
  0.0 23.8 jit_solution(12095185749761792502)
XLA Ops:
  0.0 22.3 %main.1 = (bf16[6,128,512]{2,1,0:T(8,128)(2,1)S(1)}, f32[6,512,128]{2,1,0:T(8,128)S(1)}, f32[6,8,128]{2,1,0:T(8,128)S(1)}, s32[6,8,512]{2,1,0:T(8,128)S(1)}, bf16[512,512]{1,0:T(8,128)(2,1)S(1)}) custom-call(bf16[6,128,512]{2,1,0:T(8,128)(2,1)} %bitcast.7, s32[1,6,1,128]{3,2,1,0:T(1,128)} %order_hbm.1, s32[1,6,1,26]{3,2,1,0:T(1,128)} %masks_hbm.1, ...), custom_call_target="tpu_custom_call" | custom-call | flops 9663676416 | bytes 8388608 | tf_op jit(solution)/shard_map/main/pallas_call | solution.py:379
  22.3 1.5 %tail.1 = bf16[6,128,512]{2,1,0:T(8,128)(2,1)} custom-call(f32[6,512,128]{2,1,0:T(8,128)S(1)} %get-tuple-element.10.acc_ref, f32[6,8,128]{2,1,0:T(8,128)S(1)} %get-tuple-element.11.l_ref, bf16[6,128,512]{2,1,0:T(8,128)(2,1)S(1)} %get-tuple-element.12.tiled_ref, s32[6,8,512]{2,1,0:T(8,128)S(1)} %get-tuple-element.13.live_ref, ...), custom_call_target="tpu_custom_call" | custom-call | flops 402653184 | bytes 2097152 | tf_op jit(solution)/shard_map/tail/pallas_call | solution.py:429

commit v3 on v2

--- a/solution.py
+++ b/solution.py
@@ -10,6 +10,8 @@
 HEADS = 8
 TILE = 256
 NEG = -1e30
+OFF = -3e30
+ONES = 16
 MESH = pl.DeviceIdType.MESH
 
 
@@ -40,20 +42,20 @@
     return (k, 0) if bz == 1 else (k // bz, k % bz)
 
 
-def arrange(order_ref, pts_ref, k, bz, gain_ref, shift_ref):
-    p = pts_ref.shape[1]
+def chosen(order_ref, k, bz, p):
     j, l = spot(k, bz)
     row = order_ref[0, j, pl.ds(l, 1), :]
     pick = lax.broadcasted_iota(jnp.int32, (p, p), 0) == row
-    pick = jnp.where(pick, 1.0, 0.0).astype(jnp.bfloat16)
-    tiled = lax.dot_general(
-        pick, pts_ref[k], (((0,), (0,)), ((), ())), preferred_element_type=jnp.float32
-    )
-    mean = jnp.mean(tiled, axis=-1, keepdims=True)
-    away = tiled - mean
+    return jnp.where(pick, 1.0, 0.0).astype(jnp.bfloat16)
+
+
+def norm(values, gain_ref, shift_ref):
+    values = values.astype(jnp.float32)
+    mean = jnp.mean(values, axis=-1, keepdims=True)
+    away = values - mean
     var = jnp.mean(away * away, axis=-1, keepdims=True)
     normed = away * lax.rsqrt(var + 1e-05) * gain_ref[...] + shift_ref[...]
-    return tiled.astype(jnp.bfloat16), normed.astype(jnp.bfloat16)
+    return normed.astype(jnp.bfloat16)
 
 
 def project(normed_ref, w_ref, lo, hi, put):
@@ -73,7 +75,7 @@
     return put
 
 
-def flow(rounds, items, kv_ref, qd_ref, s_ref, limit_ref, m_ref, l_ref, acc_ref, width, p):
+def flow(rounds, items, kv_ref, pick_ref, qd_ref, tag_ref, s_ref, on_ref, m_ref, l_ref, acc_ref, width, p):
     hd = width // HEADS
     pairs = HEADS // 2
 
@@ -82,45 +84,45 @@
 
     def scores(item, i):
         s, k, g, at = item
-        place = lax.broadcasted_iota(jnp.int32, (p, 2 * p), 0)
-        bias = jnp.where(place < limit_ref[at], 0.0, NEG)
-        keys = kv_ref[s, k, :, 2 * i * hd : 2 * (i + 1) * hd]
-        return jnp.dot(keys, qd_ref[g, i], preferred_element_type=jnp.float32) + bias
-
-    def soften(state, i, s):
-        tops, sums = state
-        old = lanes_of(tops, i)
-        top = jnp.maximum(old, jnp.max(s, axis=0, keepdims=True))
+        keys = jnp.concatenate(
+            [kv_ref[s, k, :, 2 * i * hd : 2 * (i + 1) * hd], pick_ref[s, k]], axis=1
+        )
+        asked = jnp.concatenate([qd_ref[g, i], tag_ref[s, k]], axis=0)
+        return jnp.dot(keys, asked, preferred_element_type=jnp.float32)
+
+    def soften(item, state, i, s):
+        off = jnp.where(on_ref[item[3]] == 1, 0.0, OFF)
+        old = lanes_of(state, i)
+        top = jnp.maximum(old, jnp.max(s, axis=0, keepdims=True) + off)
         keep = jnp.exp(old - top)
-        e = jnp.exp(s - top)
-        mass = lanes_of(sums, i) * keep + jnp.sum(e, axis=0, keepdims=True)
-        return top, mass, keep, e.astype(jnp.bfloat16)
+        e = jnp.exp(s - (top - off))
+        return top, keep, e.astype(jnp.bfloat16)
 
     def mix(item, i, e):
         values = kv_ref[item[0], item[1], :, width + 2 * i * hd : width + 2 * (i + 1) * hd]
-        return lax.dot_general(
-            values, e, (((0,), (0,)), ((), ())), preferred_element_type=jnp.float32
-        )
+        lines = jnp.concatenate([values.T, jnp.ones((ONES, p), jnp.bfloat16)], axis=0)
+        return jnp.dot(lines, e, preferred_element_type=jnp.float32)
 
     def put(item, i, soft, out):
         g = item[2]
-        top, mass, keep, _ = soft
+        top, keep, _ = soft
+        mass = out[2 * hd : 2 * hd + 1, :]
         for k in range(2):
             h = 2 * i + k
             lanes = slice(k * p, (k + 1) * p)
             down = slice(h * hd, (h + 1) * hd)
             old = acc_ref[g, down, :] * keep[:, lanes]
             acc_ref[g, down, :] = old + out[k * hd : (k + 1) * hd, lanes]
-            l_ref[g, h : h + 1, :] = mass[:, lanes]
+            l_ref[g, h : h + 1, :] = l_ref[g, h : h + 1, :] * keep[:, lanes] + mass[:, lanes]
             m_ref[g, h : h + 1, :] = top[:, lanes]
 
     def finish(item, read, ahead):
-        state = m_ref[item[2]], l_ref[item[2]]
+        state = m_ref[item[2]]
         last = None
         for i in range(pairs):
             ahead(i)
-            soft = soften(state, i, read(i))
-            out = mix(item, i, soft[3])
+            soft = soften(item, state, i, read(i))
+            out = mix(item, i, soft[2])
             if last is not None:
                 put(item, *last)
             last = (i, soft, out)
@@ -157,8 +159,8 @@
 
 
 def main_kernel(dims, pts_hbm, order_hbm, masks_hbm, counts_hbm, gain_hbm, shift_hbm, w_hbm,
-                w_out_hbm, tiled_ref, acc_ref, l_ref, live_ref, w_out_ref, pts_ref, order_ref,
-                normed_ref, block_ref, kv_ref, qd_ref, s_ref, m_ref, gain_ref, shift_ref, w_ref, limit_ref,
+                w_out_hbm, tiled_ref, acc_ref, l_ref, live_ref, w_out_ref, done_ref, pts_ref, order_ref,
+                attn_ref, normed_ref, block_ref, kv_ref, pick_ref, qd_ref, tag_ref, s_ref, m_ref, gain_ref, shift_ref, w_ref, on_ref,
                 masks_ref, counts_ref, sems, own_sem, pair_send, pair_recv, far_send, far_recv):
     by, bz, p, width, n = dims
     nb = by * bz
@@ -223,26 +225,27 @@
     near = reach(by, bz)
     reachable = len(near)
     here = has.astype(jnp.int32)
-    slabs = [(me, 0, 1), (pair, 1 - 2 * odd, 1), ((far + n) % n, 2 * odd - 1, here)]
-    for s, (at, _, there) in enumerate(slabs):
+    slabs = [(me, 1), (pair, 1), ((far + n) % n, here)]
+    row = lax.broadcasted_iota(jnp.int32, (p, 2 * p), 0)
+    lane = lax.broadcasted_iota(jnp.int32, (p, p), 1)
+    same = jnp.where(lax.broadcasted_iota(jnp.int32, (p, p), 0) == lane, 1.0, 0.0)
+    for s, (at, there) in enumerate(slabs):
         for g in range(nb):
             j, l = spot(g, bz)
+            tag_ref[s, g] = jnp.where(row < counts_ref[j, l, at], 0.0, NEG).astype(jnp.bfloat16)
+            if s == 0:
+                pick_ref[0, g] = same.astype(jnp.bfloat16)
             for r, (b, c) in enumerate(near):
                 inside = 0 <= j + b < by and 0 <= l + c < bz
-                k = g + b * bz + c
-                key = g if s < 2 else k % nb
-                slot = (s * nb + key) * reachable + r
-                if not inside:
-                    limit_ref[slot] = 0
-                    continue
-                count = counts_ref[j + b, l + c, at] * there
-                if s == 0 and (b, c) != (0, 0):
-                    count = count * masks_ref[0, j, l, column_of(0, b, c)]
-                if s > 0:
+                key = g if s < 2 else (g + b * bz + c) % nb
+                on = there if inside else 0
+                if inside and s == 0 and (b, c) != (0, 0):
+                    on = masks_ref[0, j, l, column_of(0, b, c)]
+                if inside and s > 0:
                     plus, minus = column_of(1, b, c), column_of(-1, b, c)
                     sign = 1 - odd if s == 1 else odd
-                    count = count * masks_ref[0, j, l, minus + (plus - minus) * sign]
-                limit_ref[slot] = count
+                    on = masks_ref[0, j, l, minus + (plus - minus) * sign] * there
+                on_ref[(s * nb + key) * reachable + r] = on
     for g in range(nb):
         j, l = spot(g, bz)
         live_ref[g] = jnp.full(live_ref.shape[1:], counts_ref[j, l, me], jnp.int32)
@@ -252,9 +255,12 @@
 
     own.wait()
     for g in range(nb):
-        tiled, normed = arrange(order_ref.at[0], pts_ref.at[0], g, bz, gain_ref, shift_ref)
-        tiled_ref[g] = tiled
-        normed_ref[g * p : (g + 1) * p, :] = normed
+        tiled = lax.dot_general(
+            chosen(order_ref.at[0], g, bz, p), pts_ref[0, g], (((0,), (0,)), ((), ())),
+            preferred_element_type=jnp.float32,
+        )
+        tiled_ref[g] = tiled.astype(jnp.bfloat16)
+        normed_ref[g * p : (g + 1) * p, :] = norm(tiled, gain_ref, shift_ref)
     weights.wait()
     weights_out.wait()
     blank = jnp.zeros((hd, p), jnp.bfloat16)
@@ -271,7 +277,7 @@
 
     project(normed_ref, w_ref, 0, width, put_q)
     project(normed_ref, w_ref, width, 3 * width, put_keys(kv_ref, 0, width))
-    rest = (kv_ref, qd_ref, s_ref, limit_ref, m_ref, l_ref, acc_ref, width, p)
+    rest = (kv_ref, pick_ref, qd_ref, tag_ref, s_ref, on_ref, m_ref, l_ref, acc_ref, width, p)
 
     def around(s):
         def items(g):
@@ -290,16 +296,15 @@
     pair_order.wait_recv()
     pair_points.wait_recv()
     for g in range(nb):
-        _, normed = arrange(order_ref.at[1], pts_ref.at[1], g, bz, gain_ref, shift_ref)
-        normed_ref[g * p : (g + 1) * p, :] = normed
+        pick_ref[1, g] = chosen(order_ref.at[1], g, bz, p)
+        normed_ref[g * p : (g + 1) * p, :] = norm(pts_ref[1, g], gain_ref, shift_ref)
     project(normed_ref, w_ref, width, 3 * width, put_keys(kv_ref, 1, width))
     flow(*around(1), *rest)
 
-    def fetch(k, between):
+    def fetch(k):
         far_block(k).wait_recv()
-        _, normed = arrange(order_ref.at[2], pts_ref.at[2], k, bz, gain_ref, shift_ref)
-        block_ref[...] = normed
-        between()
+        pick_ref[2, k] = chosen(order_ref.at[2], k, bz, p)
+        block_ref[...] = norm(pts_ref[2, k], gain_ref, shift_ref)
         for col in range(width, 3 * width, TILE):
             part = jnp.dot(
                 block_ref[...], w_ref[:, col : col + TILE], preferred_element_type=jnp.float32
@@ -315,15 +320,20 @@
     @pl.when(has)
     def _():
         far_order.wait_recv()
-        fetch(0, lambda: None)
-        if nb > 1:
-            fetch(1, lambda: served(0))
 
         def step(k, carry):
-            fetch(k, lambda: served(k - 1))
+            fetch(k)
+            served(k)
             return carry
 
-        lax.fori_loop(2, nb, step, 0)
+        lax.fori_loop(0, nb - 1, step, 0)
+
+    early = range(settled(by, bz))
+    close(early, early, dims, acc_ref, l_ref, tiled_ref, live_ref, w_out_ref, attn_ref, done_ref)
+
+    @pl.when(has)
+    def _():
+        fetch(nb - 1)
         served(nb - 1)
         far_order.wait_send()
         for k in range(nb):
@@ -333,33 +343,50 @@
     pair_points.wait_send()
 
 
-def tail_kernel(dims, acc_ref, l_ref, tiled_ref, live_ref, w_out_ref, out_hbm, attn_ref, out_ref, sems):
+def settled(by, bz):
+    return max(by * bz - 1 - max(b * bz + c for b, c in reach(by, bz)), 0)
+
+
+def close(some, slots, dims, acc_ref, l_ref, tiled_ref, live_ref, w_out_ref, attn_ref, out_ref):
+    by, bz, p, width, n = dims
+    if not some:
+        return
+    hd = width // HEADS
+    row = lax.broadcasted_iota(jnp.int32, (p, width), 0)
+    for t, g in enumerate(some):
+        inverse = 1.0 / l_ref[g]
+        parts = [
+            (acc_ref[g, h * hd : (h + 1) * hd, :] * inverse[h : h + 1, :]).astype(jnp.bfloat16)
+            for h in range(HEADS)
+        ]
+        attn_ref[t * p : (t + 1) * p, :] = jnp.concatenate(parts, axis=0).T
+    mixed = jnp.dot(
+        attn_ref[: len(some) * p, :], w_out_ref[...], preferred_element_type=jnp.float32
+    )
+    for t, (g, slot) in enumerate(zip(some, slots)):
+        part = mixed[t * p : (t + 1) * p] + tiled_ref[g].astype(jnp.float32)
+        part = jnp.where(row < live_ref[g, :1, :], part, 0.0)
+        out_ref[slot] = part.astype(jnp.bfloat16)
+
+
+def tail_kernel(dims, acc_ref, l_ref, tiled_ref, live_ref, w_out_ref, done_ref, out_hbm, attn_ref,
+                out_ref, sems):
     by, bz, p, width, n = dims
     nb = by * bz
-    hd = width // HEADS
-    row = lax.broadcasted_iota(jnp.int32, (p, width), 0)
+    early = settled(by, bz)
     ends = []
-    for lo in range(0, nb, 3):
-        some = range(lo, min(lo + 3, nb))
-        for g in some:
-            inverse = 1.0 / l_ref[g]
-            parts = [
-                (acc_ref[g, h * hd : (h + 1) * hd, :] * inverse[h : h + 1, :]).astype(jnp.bfloat16)
-                for h in range(HEADS)
-            ]
-            attn_ref[g * p : (g + 1) * p, :] = jnp.concatenate(parts, axis=0).T
-        mixed = jnp.dot(
-            attn_ref[lo * p : (lo + len(some)) * p, :], w_out_ref[...],
-            preferred_element_type=jnp.float32,
-        )
-        for k, g in enumerate(some):
-            part = mixed[k * p : (k + 1) * p] + tiled_ref[g].astype(jnp.float32)
-            part = jnp.where(row < live_ref[g, :1, :], part, 0.0)
-            out_ref[g] = part.astype(jnp.bfloat16)
-        held = pl.ds(lo, len(some))
-        end = pltpu.make_async_copy(out_ref.at[held], out_hbm.at[held], sems.at[lo // 3])
+
+    def send(source, lo, size):
+        end = pltpu.make_async_copy(source, out_hbm.at[pl.ds(lo, size)], sems.at[len(ends)])
         end.start()
         ends.append(end)
+
+    if early:
+        send(done_ref, 0, early)
+    late = range(early, nb)
+    close(late, range(len(late)), dims, acc_ref, l_ref, tiled_ref, live_ref, w_out_ref, attn_ref,
+          out_ref)
+    send(out_ref, early, len(late))
     for end in ends:
         end.wait()
 
@@ -376,7 +403,8 @@
     vmem = pl.BlockSpec(memory_space=pltpu.VMEM)
     hbm = pl.BlockSpec(memory_space=pltpu.HBM)
     half = jnp.bfloat16
-    tiled, acc, sums, live, w_here = pl.pallas_call(
+    early = settled(by, bz)
+    tiled, acc, sums, live, w_here, done = pl.pallas_call(
         functools.partial(main_kernel, dims),
         name="main",
         out_shape=[
@@ -385,16 +413,20 @@
             shape((nb, HEADS, p), jnp.float32),
             shape((nb, 8, width), jnp.int32),
             shape(w_out.shape, half),
+            shape((max(early, 1), p, width), half),
         ],
         in_specs=[hbm] * 8,
-        out_specs=[vmem] * 5,
+        out_specs=[vmem] * 6,
         scratch_shapes=[
             pltpu.VMEM((3, nb, p, width), half),
             pltpu.VMEM((3,) + order.shape, jnp.int32),
+            pltpu.VMEM((max(early, 1) * p, width), half),
             pltpu.VMEM((nb * p, width), half),
             pltpu.VMEM((p, width), half),
             pltpu.VMEM((3, nb, p, 2 * width), half),
+            pltpu.VMEM((3, nb, p, p), half),
             pltpu.VMEM((nb, HEADS // 2, width // HEADS * 2, 2 * p), half),
+            pltpu.VMEM((3, nb, p, 2 * p), half),
             pltpu.VMEM((HEADS // 2, p, 2 * p), jnp.float32),
             pltpu.VMEM((nb, HEADS, p), jnp.float32),
             pltpu.VMEM((1, width), jnp.float32),
@@ -430,18 +462,18 @@
         functools.partial(tail_kernel, dims),
         name="tail",
         out_shape=shape((nb, p, width), half),
-        in_specs=[vmem] * 5,
+        in_specs=[vmem] * 6,
         out_specs=hbm,
         scratch_shapes=[
-            pltpu.VMEM((nb * p, width), half),
-            pltpu.VMEM((nb, p, width), half),
-            dma((-(-nb // 3),)),
+            pltpu.VMEM(((nb - early) * p, width), half),
+            pltpu.VMEM((nb - early, p, width), half),
+            dma((2,)),
         ],
         cost_estimate=pl.CostEstimate(
-            flops=2 * nb * p * width * width, transcendentals=0, bytes_accessed=2 << 20
+            flops=2 * (nb - early) * p * width * width, transcendentals=0, bytes_accessed=2 << 20
         ),
         compiler_params=pltpu.CompilerParams(vmem_limit_bytes=16 << 20),
-    )(acc, sums, tiled, live, w_here)
+    )(acc, sums, tiled, live, w_here, done)
     return out.reshape(points.shape)
 
 

time: 23.9 us -> 22.9 us (0.958)
  Pallas kernels: 23.8 us -> 22.7 us
    pallas_call x1, Pallas kernels: 22.3 us -> 21.7 us  [shards(): pl.pallas_call(functools.partial(main_kernel, dims), name='main', out_sha...]
    pallas_call x1, Pallas kernels: 1.46 us -> 1.07 us  [shards(): pl.pallas_call(functools.partial(tail_kernel, dims), name='tail', out_sha...]
where the time goes in v3:
time: 22.9 us; the launch traced here: 22.8 us
  Pallas kernels  22.7 us (99%)
    pallas_call x1, Pallas kernels, shards(): pl.pallas_call(functools.partial(main_kernel, dims), name='main', out_sha...  21.7 us
    pallas_call x1, Pallas kernels, shards(): pl.pallas_call(functools.partial(tail_kernel, dims), name='tail', out_sha...  1.07 us

profile of v3, /device:TPU:25, one launch (start us, length us, event | category | flops | bytes accessed | tf_op | source)
XLA Modules:
  0.0 22.8 jit_solution(9257895267913056466)
XLA Ops:
  0.0 21.7 %main.1 = (bf16[6,128,512]{2,1,0:T(8,128)(2,1)S(1)}, f32[6,512,128]{2,1,0:T(8,128)S(1)}, f32[6,8,128]{2,1,0:T(8,128)S(1)}, s32[6,8,512]{2,1,0:T(8,128)S(1)}, bf1...) custom-call(bf16[6,128,512]{2,1,0:T(8,128)(2,1)} %bitcast.7, s32[1,6,1,128]{3,2,1,0:T(1,128)} %order_hbm.1, ...), custom_call_target="tpu_custom_call" | custom-call | flops 9663676416 | bytes 8388608 | tf_op jit(solution)/shard_map/main/pallas_call | solution.py:407
  21.7 1.1 %tail.1 = bf16[6,128,512]{2,1,0:T(8,128)(2,1)} custom-call(f32[6,512,128]{2,1,0:T(8,128)S(1)} %get-tuple-element.11.acc_ref, f32[6,8,128]{2,1,0:T(8,128)S(1)} %get-tuple-element.12.l_ref, bf16[6,128,512]{2,1,0:T(8,128)(2,1)S(1)} %get-tuple-element.13.tiled_ref, s32[6,8,512]{2,1,0:T(8,128)S(1)} %get-tuple-element.14.live_ref, ...), custom_call_target="tpu_custom_call" | custom-call | flops 134217728 | bytes 2097152 | tf_op jit(solution)/shard_map/tail/pallas_call | solution.py:461

commit v4 on v3

--- a/solution.py
+++ b/solution.py
@@ -213,8 +213,9 @@
 
     @pl.when(has)
     def _():
+        far_block(0).start()
         far_order.start()
-        for k in range(nb):
+        for k in range(1, nb):
             far_block(k).start()
 
     pair_order.start()
@@ -383,10 +384,10 @@
 
     if early:
         send(done_ref, 0, early)
-    late = range(early, nb)
-    close(late, range(len(late)), dims, acc_ref, l_ref, tiled_ref, live_ref, w_out_ref, attn_ref,
-          out_ref)
-    send(out_ref, early, len(late))
+    for t, g in enumerate(range(early, nb)):
+        close([g], [t], dims, acc_ref, l_ref, tiled_ref, live_ref, w_out_ref,
+              attn_ref.at[pl.ds(t * p, p)], out_ref)
+        send(out_ref.at[pl.ds(t, 1)], g, 1)
     for end in ends:
         end.wait()
 
@@ -467,7 +468,7 @@
         scratch_shapes=[
             pltpu.VMEM(((nb - early) * p, width), half),
             pltpu.VMEM((nb - early, p, width), half),
-            dma((2,)),
+            dma((1 + nb - early,)),
         ],
         cost_estimate=pl.CostEstimate(
             flops=2 * (nb - early) * p * width * width, transcendentals=0, bytes_accessed=2 << 20

time: 22.9 us -> 22.9 us (level)
  no operation moved by 1% of the time
where the time goes in v4:
time: 22.9 us; the launch traced here: 22.7 us
  Pallas kernels  22.7 us (99%)
    pallas_call x1, Pallas kernels, shards(): pl.pallas_call(functools.partial(main_kernel, dims), name='main', out_sha...  21.7 us
    pallas_call x1, Pallas kernels, shards(): pl.pallas_call(functools.partial(tail_kernel, dims), name='tail', out_sha...  1.03 us

profile of v4, /device:TPU:25, one launch (start us, length us, event | category | flops | bytes accessed | tf_op | source)
XLA Modules:
  0.0 22.7 jit_solution(14874112446026970765)
XLA Ops:
  0.0 21.7 %main.1 = (bf16[6,128,512]{2,1,0:T(8,128)(2,1)S(1)}, f32[6,512,128]{2,1,0:T(8,128)S(1)}, f32[6,8,128]{2,1,0:T(8,128)S(1)}, s32[6,8,512]{2,1,0:T(8,128)S(1)}, bf1...) custom-call(bf16[6,128,512]{2,1,0:T(8,128)(2,1)} %bitcast.7, s32[1,6,1,128]{3,2,1,0:T(1,128)} %order_hbm.1, ...), custom_call_target="tpu_custom_call" | custom-call | flops 9663676416 | bytes 8388608 | tf_op jit(solution)/shard_map/main/pallas_call | solution.py:408
  21.7 1.0 %tail.1 = bf16[6,128,512]{2,1,0:T(8,128)(2,1)} custom-call(f32[6,512,128]{2,1,0:T(8,128)S(1)} %get-tuple-element.11.acc_ref, f32[6,8,128]{2,1,0:T(8,128)S(1)} %get-tuple-element.12.l_ref, bf16[6,128,512]{2,1,0:T(8,128)(2,1)S(1)} %get-tuple-element.13.tiled_ref, s32[6,8,512]{2,1,0:T(8,128)S(1)} %get-tuple-element.14.live_ref, ...), custom_call_target="tpu_custom_call" | custom-call | flops 134217728 | bytes 2097152 | tf_op jit(solution)/shard_map/tail/pallas_call | solution.py:462

commit v5 on v4

--- a/solution.py
+++ b/solution.py
@@ -327,15 +327,16 @@
             served(k)
             return carry
 
-        lax.fori_loop(0, nb - 1, step, 0)
+        lax.fori_loop(0, nb - 2, step, 0)
 
     early = range(settled(by, bz))
     close(early, early, dims, acc_ref, l_ref, tiled_ref, live_ref, w_out_ref, attn_ref, done_ref)
 
     @pl.when(has)
     def _():
-        fetch(nb - 1)
-        served(nb - 1)
+        for k in range(max(nb - 2, 0), nb):
+            fetch(k)
+            served(k)
         far_order.wait_send()
         for k in range(nb):
             far_block(k).wait_send()
@@ -345,7 +346,7 @@
 
 
 def settled(by, bz):
-    return max(by * bz - 1 - max(b * bz + c for b, c in reach(by, bz)), 0)
+    return max(by * bz - 2 - max(b * bz + c for b, c in reach(by, bz)), 0)
 
 
 def close(some, slots, dims, acc_ref, l_ref, tiled_ref, live_ref, w_out_ref, attn_ref, out_ref):

time: 22.9 us -> 22.8 us (level)
  no operation moved by 1% of the time
where the time goes in v5:
time: 22.8 us; the launch traced here: 22.6 us
  Pallas kernels  22.6 us (99%)
    pallas_call x1, Pallas kernels, shards(): pl.pallas_call(functools.partial(main_kernel, dims), name='main', out_sha...  21.5 us
    pallas_call x1, Pallas kernels, shards(): pl.pallas_call(functools.partial(tail_kernel, dims), name='tail', out_sha...  1.11 us

profile of v5, /device:TPU:25, one launch (start us, length us, event | category | flops | bytes accessed | tf_op | source)
XLA Modules:
  0.0 22.6 jit_solution(16478864348510246068)
XLA Ops:
  0.0 21.5 %main.1 = (bf16[6,128,512]{2,1,0:T(8,128)(2,1)S(1)}, f32[6,512,128]{2,1,0:T(8,128)S(1)}, f32[6,8,128]{2,1,0:T(8,128)S(1)}, s32[6,8,512]{2,1,0:T(8,128)S(1)}, bf1...) custom-call(bf16[6,128,512]{2,1,0:T(8,128)(2,1)} %bitcast.7, s32[1,6,1,128]{3,2,1,0:T(1,128)} %order_hbm.1, ...), custom_call_target="tpu_custom_call" | custom-call | flops 9663676416 | bytes 8388608 | tf_op jit(solution)/shard_map/main/pallas_call | solution.py:409
  21.5 1.1 %tail.1 = bf16[6,128,512]{2,1,0:T(8,128)(2,1)} custom-call(f32[6,512,128]{2,1,0:T(8,128)S(1)} %get-tuple-element.11.acc_ref, f32[6,8,128]{2,1,0:T(8,128)S(1)} %get-tuple-element.12.l_ref, bf16[6,128,512]{2,1,0:T(8,128)(2,1)S(1)} %get-tuple-element.13.tiled_ref, s32[6,8,512]{2,1,0:T(8,128)S(1)} %get-tuple-element.14.live_ref, ...), custom_call_target="tpu_custom_call" | custom-call | flops 201326592 | bytes 2097152 | tf_op jit(solution)/shard_map/tail/pallas_call | solution.py:463
